TPU v7x, 32 devices: a whole 2x2x4 slice. The times are simulated.
32 devices in a mesh: section: 4 (over y, core), sim: 8 (over z, x).
Axes of the slice: x: 2, y: 2, z: 4, core: 2. Of those that a mesh axis runs over, the one named last changes fastest.
Arguments:
- state: float32 [128, 64, 8192], P('section', None, 'sim'), may hold values from -60 to 60
- owner: int32 [128, 1], P('section'), may hold values from 0 to 7; in each aligned block of 32 rows (0 to 31, 32 to 63, ...) at most 8 rows name the same one
- counts: int32 [128], P('section'), may hold values from 2048 to 8192
Outputs:
- slab_mean: float32 [128, 64], P('section')
- slab_cov: float32 [128, 4096], P('section', 'sim')
- group_cov: float32 [32, 4096], P(('section', 'sim'))
- global_mean: float32 [64], replicated
- global_cov: float32 [64, 64], replicated
Inputs may be any that keep to these rules, and one draw needn't show every extreme that they name: Among the 32 slabs of one group, no owner is named by more than 8 slabs, and one owner is named by exactly 8 slabs in some or all groups.
All inputs are finite; a program needn't handle non-finite values.
Results may differ from a plain program's by a relative error of at most 0.0003.
Values sent between devices are 32-bit elements; how exact they have to be, the bound alone decides.
A program may use at most 64 MiB of HBM per device.

v0:
```python
import jax
import jax.numpy as jnp
from jax import lax
from jax.sharding import PartitionSpec as P


def slot_payload(number, mean, comoment, capacity, n_sim, width):
    slot_cov = comoment / jnp.maximum(number - 1.0, 1.0)[:, None]
    cov_parts = slot_cov.reshape(capacity, n_sim, width * width // n_sim)
    mean_copies = jnp.broadcast_to(mean[:, None, :], (capacity, n_sim, width))
    return (cov_parts, mean_copies)


def owner_stats(number, mean, comoment):
    high = lax.Precision.HIGHEST
    width = mean.shape[1]
    group_count = jnp.sum(number)
    group_mean = jnp.sum(number[:, None] * mean, axis=0) / jnp.maximum(group_count, 1.0)
    offset = mean - group_mean[None, :]
    group_co = jnp.sum(comoment, axis=0) + jnp.einsum(
        "k,kv,kw->vw", number, offset, offset, precision=high
    ).reshape(width * width)
    return (group_count, group_mean, group_co)


def local(state, owner, counts):
    high = lax.Precision.HIGHEST
    slab_here, width, cells_dev = state.shape
    n_sim = lax.axis_size("sim")
    my_index = lax.axis_index("sim")
    capacity = 2 * slab_here // n_sim
    slots = n_sim * capacity
    target = owner[:, 0]
    order = jnp.arange(slab_here, dtype=jnp.int32)
    earlier = (target[:, None] == target[None, :]) & (order[None, :] < order[:, None])
    rank = jnp.sum(earlier.astype(jnp.int32), axis=1)
    slot_of = target * capacity + rank
    match = slot_of[:, None] == jnp.arange(slots, dtype=jnp.int32)[None, :]
    filled = jnp.any(match, axis=0)
    source_slab = jnp.sum(jnp.where(match, order[:, None], 0), axis=0)
    tile_start = my_index * cells_dev
    tile_count = jnp.clip(counts - tile_start, 0, cells_dev).astype(jnp.float32)
    live = jnp.arange(cells_dev, dtype=jnp.int32)[None, :] + tile_start < counts[:, None]
    tile_mean = (
        jnp.sum(jnp.where(live[:, None, :], state, 0.0), axis=2)
        / jnp.maximum(tile_count, 1.0)[:, None]
    )
    centered = jnp.where(live[:, None, :], state - tile_mean[:, :, None], 0.0)
    tile_co = jnp.einsum("svc,swc->svw", centered, centered, precision=high).reshape(
        slab_here, width * width
    )
    send_mean = jnp.where(filled[:, None], tile_mean[source_slab], 0.0).reshape(
        n_sim, capacity, width
    )
    send_co = jnp.where(filled[:, None], tile_co[source_slab], 0.0).reshape(
        n_sim, capacity, width * width
    )
    send_count = jnp.where(filled, tile_count[source_slab], 0.0).reshape(n_sim, capacity)
    means = lax.all_to_all(send_mean, "sim", split_axis=0, concat_axis=0, tiled=True)
    comoms = lax.all_to_all(send_co, "sim", split_axis=0, concat_axis=0, tiled=True)
    amounts = lax.all_to_all(send_count, "sim", split_axis=0, concat_axis=0, tiled=True)
    number = jnp.sum(amounts, axis=0)
    mean = jnp.sum(amounts[:, :, None] * means, axis=0) / jnp.maximum(number, 1.0)[:, None]
    offset = means - mean[None, :, :]
    extra = jnp.einsum("ik,ikv,ikw->kvw", amounts, offset, offset, precision=high)
    number, mean, comoment = (
        number,
        mean,
        jnp.sum(comoms, axis=0) + extra.reshape(number.shape[0], width * width),
    )
    cov_parts, mean_copies = slot_payload(number, mean, comoment, capacity, n_sim, width)
    back_cov, back_mean = (
        lax.all_to_all(cov_parts, "sim", split_axis=1, concat_axis=0, tiled=True),
        lax.all_to_all(mean_copies, "sim", split_axis=1, concat_axis=0, tiled=True),
    )
    slab_cov = back_cov[slot_of, 0]
    slab_mean = back_mean[slot_of, 0]
    group_count, group_mean, group_co = owner_stats(number, mean, comoment)
    group_cov = (group_co / jnp.maximum(group_count - 1.0, 1.0))[None, :]
    total, weighted = lax.psum((group_count, group_count * group_mean), ("section", "sim"))
    global_mean = weighted / total
    gap = group_mean - global_mean
    spread = lax.psum(group_co + group_count * jnp.outer(gap, gap).reshape(-1), ("section", "sim"))
    global_cov = (spread / (total - 1.0)).reshape(width, width)
    return (slab_mean, slab_cov, group_cov, global_mean, global_cov)


def solution(mesh):
    return jax.shard_map(
        local,
        mesh=mesh,
        in_specs=(P("section", None, "sim"), P("section", None), P("section")),
        out_specs=(P("section", None), P("section", "sim"), P(("section", "sim"), None), P(), P()),
        check_vma=False,
    )
```

profile of v0, /device:TPU:0, one launch (start us, length us, event | category | flops | bytes accessed | tf_op | source)
XLA Modules:
  0.0 160.8 jit_solution(15916009984353185825)
XLA Ops:
  0.6 0.9 convert_reduce_fusion
  3.1 0.8 gather_fusion
  4.5 7.3 %all-to-all-start = ((f32[8,1,8]{2,1,0:T(1,128)}), f32[8,1,8]{2,1,0:T(1,128)S(1)}, u32[]{:S(2)}, u32[]{:S(2)}) async-start(f32[8,1,8]{2,1,0:T(1,128)} %bitcast.5), calls=%async_computation | async-start | bytes 8192 | tf_op jit(solution)/shard_map/all_to_all | solution.py:61
  11.9 0.7 broadcast_compare_fusion
  12.7 4.1 %select_reduce_fusion = f32[32,64]{1,0:T(8,128)S(1)} fusion(f32[32,64,1024]{2,1,0:T(8,128)} %param.3, pred[32,1024]{1,0:T(8,128)(4,1)S(1)} %broadcast_compare_fusion), kind=kLoop, calls=%fused_computation.8 | loop fusion | flops 4192256 | bytes 8429568 | tf_op jit(solution)/shard_map/reduce_sum | solution.py:45
  17.5 14.9 %fusion = f32[32,64,64]{2,1,0:T(8,128)S(1)} fusion(f32[32,64,1024]{2,1,0:T(8,128)} %param.3, f32[32,64]{1,0:T(8,128)S(1)} %broadcast_divide_fusion.2, pred[32,1024]{1,0:T(8,128)(4,1)S(1)} %broadcast_compare_fusion), kind=kOutput, calls=%fused_computation.5 | convolution fusion | flops 1614807040 | bytes 8953856 | tf_op jit(solution)/shard_map/svc,swc->svw/dot_general | solution.py:49
  32.5 0.7 reshape.244
  33.5 0.9 gather_fusion.3
  34.5 6.0 %all-to-all-start.1 = ((f32[8,1,512]{2,1,0:T(1,128)}), f32[8,1,512]{2,1,0:T(1,128)S(1)}, u32[]{:S(2)}, u32[]{:S(2)}) async-start(f32[8,1,512]{2,1,0:T(1,128)} %reshape.244), calls=%async_computation.1 | async-start | bytes 32768 | tf_op jit(solution)/shard_map/all_to_all | solution.py:59
  41.1 6.0 %all-to-all-done.1 = f32[8,1,512]{2,1,0:T(1,128)S(1)} async-done(((f32[8,1,512]{2,1,0:T(1,128)}), f32[8,1,512]{2,1,0:T(1,128)S(1)}, u32[]{:S(2)}, u32[]{:S(2)}) %all-to-all-start.1) | async-done | bytes 16416 | tf_op jit(solution)/shard_map/all_to_all | solution.py:59
  48.5 0.7 reshape.246
  49.2 3.3 %all-to-all-start.2 = ((f32[8,1,512]{2,1,0:T(1,128)}), f32[8,1,512]{2,1,0:T(1,128)S(1)}, u32[]{:S(2)}, u32[]{:S(2)}) async-start(f32[8,1,512]{2,1,0:T(1,128)} %reshape.246), calls=%async_computation.2 | async-start | bytes 32768 | tf_op jit(solution)/shard_map/all_to_all | solution.py:74
  52.6 1.1 bitcast_select_fusion
  53.7 5.4 %all-to-all-done.2 = f32[8,1,512]{2,1,0:T(1,128)S(1)} async-done(((f32[8,1,512]{2,1,0:T(1,128)}), f32[8,1,512]{2,1,0:T(1,128)S(1)}, u32[]{:S(2)}, u32[]{:S(2)}) %all-to-all-start.2) | async-done | bytes 16416 | tf_op jit(solution)/shard_map/all_to_all | solution.py:74
  59.1 3.6 %all-to-all-start.3 = ((f32[8,8,4096]{2,1,0:T(8,128)}), f32[8,8,4096]{2,1,0:T(8,128)S(1)}, u32[]{:S(2)}, u32[]{:S(2)}) async-start(f32[8,8,4096]{2,1,0:T(8,128)} %bitcast_select_fusion), calls=%async_computation.3 | async-start | bytes 2097152 | tf_op jit(solution)/shard_map/all_to_all | solution.py:60
  64.6 41.6 %all-reduce.1 = (f32[64]{0:T(128)S(1)}, f32[]{:T(128)}) all-reduce(f32[64]{0:T(128)S(1)} %get-tuple-element.11, f32[]{:T(128)} %get-tuple-element.5), channel_id=1, replica_groups=mesh['section'=4,'sim'=8] {'section','sim'}, use_global_device_ids=true, to_apply=%region_10.11 | all-reduce | flops 65 | bytes 520 | tf_op jit(solution)/shard_map/psum | solution.py:80
  106.8 1.2 fusion.23
  108.8 1.2 gather_fusion.2
  110.9 0.7 fusion.6
  111.7 5.3 %all-to-all-start.4 = ((f32[8,8,512]{2,0,1:T(8,128)}), f32[8,8,512]{2,0,1:T(8,128)S(1)}, u32[]{:S(2)}, u32[]{:S(2)}) async-start(f32[8,8,512]{2,0,1:T(8,128)} %fusion.6), calls=%async_computation.4 | async-start | bytes 262144 | tf_op jit(solution)/shard_map/all_to_all | solution.py:73
  117.0 1.0 multiply_add_fusion
  118.7 40.0 %psum.23 = f32[4096]{0:T(1024)S(1)} all-reduce(f32[4096]{0:T(1024)S(1)} %add.82), channel_id=1, replica_groups=mesh['section'=4,'sim'=8] {'section','sim'}, use_global_device_ids=true, to_apply=%region_12.13 | all-reduce | flops 4096 | bytes 32768 | tf_op jit(solution)/shard_map/psum | solution.py:83
  158.7 0.7 reshape.207
  159.6 1.2 gather_fusion.4
  (37 shorter events, 8.8 us)
Async XLA Ops:
  4.5 29.9 %all-to-all-start = ((f32[8,1,8]{2,1,0:T(1,128)}), f32[8,1,8]{2,1,0:T(1,128)S(1)}, u32[]{:S(2)}, u32[]{:S(2)}) async-start(f32[8,1,8]{2,1,0:T(1,128)} %bitcast.5), calls=%async_computation | async-start | bytes 8192 | tf_op jit(solution)/shard_map/all_to_all | solution.py:61
  34.5 12.6 %all-to-all-start.1 = ((f32[8,1,512]{2,1,0:T(1,128)}), f32[8,1,512]{2,1,0:T(1,128)S(1)}, u32[]{:S(2)}, u32[]{:S(2)}) async-start(f32[8,1,512]{2,1,0:T(1,128)} %reshape.244), calls=%async_computation.1 | async-start | bytes 32768 | tf_op jit(solution)/shard_map/all_to_all | solution.py:59
  49.2 9.9 %all-to-all-start.2 = ((f32[8,1,512]{2,1,0:T(1,128)}), f32[8,1,512]{2,1,0:T(1,128)S(1)}, u32[]{:S(2)}, u32[]{:S(2)}) async-start(f32[8,1,512]{2,1,0:T(1,128)} %reshape.246), calls=%async_computation.2 | async-start | bytes 32768 | tf_op jit(solution)/shard_map/all_to_all | solution.py:74
  59.1 51.0 %all-to-all-start.3 = ((f32[8,8,4096]{2,1,0:T(8,128)}), f32[8,8,4096]{2,1,0:T(8,128)S(1)}, u32[]{:S(2)}, u32[]{:S(2)}) async-start(f32[8,8,4096]{2,1,0:T(8,128)} %bitcast_select_fusion), calls=%async_computation.3 | async-start | bytes 2097152 | tf_op jit(solution)/shard_map/all_to_all | solution.py:60
  111.7 47.8 %all-to-all-start.4 = ((f32[8,8,512]{2,0,1:T(8,128)}), f32[8,8,512]{2,0,1:T(8,128)S(1)}, u32[]{:S(2)}, u32[]{:S(2)}) async-start(f32[8,8,512]{2,0,1:T(8,128)} %fusion.6), calls=%async_computation.4 | async-start | bytes 262144 | tf_op jit(solution)/shard_map/all_to_all | solution.py:73
where the time goes:
time: 162 us; the launch traced here: 161 us
  blocking collectives  81.6 us (50%)
  starting transfers between devices  25.5 us (16%)
  matrix products  16.5 us (10%)
  other arithmetic  13.4 us (8%)
  waiting for transfers between devices  11.3 us (7%)
  local copies, waits for them, and re-layouts  9.73 us (6%)
  between operations  2.71 us (2%)
    psum x1, blocking collectives, local(): lax.psum((group_count, group_count * group_mean), ('section', 'sim'))  41.6 us
    psum x1, blocking collectives, local(): lax.psum(group_co + group_count * jnp.outer(gap, gap).reshape(-1), ('sect...  40 us
    dot_general x1, matrix products, local(): jnp.einsum('svc,swc->svw', centered, centered, precision=high)  14.9 us
    all_to_all x1, starting transfers between devices, local(): lax.all_to_all(send_count, 'sim', split_axis=0, concat_axis=0, tiled=True)  7.28 us
    all_to_all x1, starting transfers between devices, local(): lax.all_to_all(send_mean, 'sim', split_axis=0, concat_axis=0, tiled=True)  6.01 us
    all_to_all x1, waiting for transfers between devices, local(): lax.all_to_all(send_mean, 'sim', split_axis=0, concat_axis=0, tiled=True)  5.96 us
    all_to_all x1, waiting for transfers between devices, local(): lax.all_to_all(mean_copies, 'sim', split_axis=1, concat_axis=0, tiled=True)  5.37 us
    all_to_all x1, starting transfers between devices, local(): lax.all_to_all(cov_parts, 'sim', split_axis=1, concat_axis=0, tiled=True)  5.31 us
  transfers between devices with their start and end apart: 5, of which 2 were waited for; matrix products, arithmetic and copies ran while one was open for 19% of the time, Pallas kernels for 0%

commit v1 on v0

v1 whole, which is shorter than its diff:
```python
import functools

import jax
import jax.numpy as jnp
from jax import lax
from jax.experimental import pallas as pl
from jax.experimental.pallas import tpu as pltpu
from jax.sharding import PartitionSpec as P

HIGH = lax.Precision.HIGHEST


def dot(a, b):
    return jnp.dot(a, b, precision=HIGH, preferred_element_type=jnp.float32)


def widen(rows, times):
    pair = jnp.concatenate([rows, rows], axis=1)
    return jnp.concatenate([pair] * (times // 2), axis=1)


def kernel(
    n_sec, n_sim, chunks,
    state, counts_s, counts_v, owner_v,
    mean_out, cov_out, gcov_out, gmean_out, glob_out,
    x, send, recv, acc, mt, mrec, psend, prec, gbuf, g64,
    in_sem, s1, r1, sm, rm, sp, rp, sg, rg,
):
    slabs, width, cells = x.shape
    half = slabs // 2
    vb = width // n_sim
    flat = vb * width
    per = half // chunks
    me = lax.axis_index("sim")
    sec = lax.axis_index("section")

    def peer(k):
        return lax.rem(me + k, n_sim)

    def source(k):
        return lax.rem(me + n_sim - k, n_sim)

    def far(a):
        return lax.rem(sec + a, n_sec)

    def back(a):
        return lax.rem(sec + n_sec - a, n_sec)

    def load(c, h):
        rows = pl.ds(h * half + c * per, per)
        return pltpu.make_async_copy(state.at[rows], x.at[rows], in_sem.at[c, h])

    for c in range(chunks):
        for h in range(2):
            load(c, h).start()

    others = [(a, k) for a in range(n_sec) for k in range(n_sim) if (a, k) != (0, 0)]
    barrier = pltpu.get_barrier_semaphore()
    for a, k in others:
        pl.semaphore_signal(
            barrier, inc=1, device_id={"section": far(a), "sim": peer(k)},
            device_id_type=pl.DeviceIdType.MESH,
        )

    def remote(src, dst, ssem, rsem, a, k):
        return pltpu.make_async_remote_copy(
            src_ref=src, dst_ref=dst, send_sem=ssem, recv_sem=rsem,
            device_id={"section": far(a), "sim": peer(k)},
            device_id_type=pl.DeviceIdType.MESH,
        )

    def piece(c, k, slot):
        rows = pl.ds(c * per, per)
        return remote(
            send.at[peer(k), rows], recv.at[slot, rows], s1.at[c, k], r1.at[c, k], 0, k
        )

    def means(k, slot):
        return remote(mrec.at[me], mrec.at[slot], sm.at[k], rm.at[k], 0, k)

    def group_piece(k, slot):
        return remote(psend.at[peer(k)], prec.at[slot], sp.at[k], rp.at[k], 0, k)

    def global_piece(a, k, slot):
        return remote(
            gbuf.at[sec * n_sim + me], gbuf.at[slot],
            sg.at[a * n_sim + k], rg.at[a * n_sim + k], a, k,
        )

    start = me * cells
    cell = lax.broadcasted_iota(jnp.int32, (1, cells), 1)
    lane = lax.broadcasted_iota(jnp.int32, (width, 2 * width), 1)
    low = lane < width

    def moments(s):
        count = counts_s[s] - start
        live = cell < count
        number = jnp.clip(count, 1, cells).astype(jnp.float32)
        block = x[s]
        mean = jnp.sum(jnp.where(live, block, 0.0), axis=1, keepdims=True) / number
        centered = jnp.where(live, block - mean, 0.0)
        top = centered.astype(jnp.bfloat16)
        rest = (centered - top.astype(jnp.float32)).astype(jnp.bfloat16)
        both = jnp.concatenate([top, rest], axis=0)
        full = lax.dot_general(
            both, both, (((1,), (1,)), ((), ())), preferred_element_type=jnp.float32
        )
        return mean, full[:width] + full[width:]

    def one_pair(p, carry):
        mean_a, a = moments(p)
        mean_b, b = moments(p + half)
        both = jnp.where(low, a, pltpu.roll(b, width, 1)) + jnp.where(
            low, pltpu.roll(a, width, 1), b
        )
        for j in range(n_sim):
            send[j, p] = both[j * vb:(j + 1) * vb]
        mt[...] = jnp.where(lane == p, mean_a, jnp.where(lane == p + half, mean_b, mt[...]))
        return carry

    mt[...] = jnp.zeros_like(mt)
    for c in range(chunks):
        for h in range(2):
            load(c, h).wait()
        lax.fori_loop(c * per, (c + 1) * per, one_pair, 0)
        if c == 0:
            pl.semaphore_wait(barrier, len(others))
        if c == chunks - 1:
            rows = jnp.transpose(mt[...])
            mrec[me] = jnp.concatenate([rows[:half], rows[half:slabs]], axis=1)
            for k in range(1, n_sim):
                means(k, me).start()
        for k in range(1, n_sim):
            piece(c, k, me).start()

    counts = counts_v[...]
    number = counts.astype(jnp.float32)
    owner = owner_v[...]
    spot = lax.broadcasted_iota(jnp.int32, (width, flat), 1)
    line = lax.broadcasted_iota(jnp.int32, (width, flat), 0)
    choose = (line == me * vb + spot // width).astype(jnp.float32)
    owner_rows = jnp.transpose(jnp.broadcast_to(owner.astype(jnp.float32), (slabs, 128)))
    name = lax.broadcasted_iota(jnp.int32, (n_sim, slabs), 0)
    member = (owner_rows[:n_sim] == name.astype(jnp.float32)).astype(jnp.float32)
    column = lax.broadcasted_iota(jnp.int32, (slabs, n_sim), 1)
    member_t = (owner == column).astype(jnp.float32)

    for k in range(1, n_sim):
        means(k, source(k)).wait_recv()
    tiles, amounts = [], []
    for j in range(n_sim):
        packed = mrec[j]
        tiles.append(jnp.concatenate([packed[:, :width], packed[:, width:]], axis=0))
        amounts.append(jnp.clip(counts - j * cells, 0, cells).astype(jnp.float32))
    mean = sum(n * t for n, t in zip(amounts, tiles)) / number
    mean_out[...] = mean
    gaps = [t - mean for t in tiles]
    picked = dot(jnp.concatenate(gaps, axis=0), choose)
    extra = sum(
        n * picked[j * slabs:(j + 1) * slabs] * widen(gaps[j], vb)
        for j, n in enumerate(amounts)
    )
    sums = dot(
        member,
        jnp.concatenate([number * mean, jnp.broadcast_to(number, (slabs, width))], axis=1),
    )
    group_count = sums[:, width:width + 1]
    group_mean = sums[:, :width] / jnp.maximum(group_count, 1.0)
    offset = mean - dot(member_t, group_mean)
    spread = number * dot(offset, choose) * widen(offset, vb)
    sec_count = jnp.sum(group_count, axis=0, keepdims=True)
    sec_mean = jnp.sum(sums[:, :width], axis=0, keepdims=True) / sec_count
    shift = group_mean - sec_mean
    sec_extra = group_count * dot(shift, choose) * widen(shift, vb)

    for k in range(1, n_sim):
        for c in range(chunks):
            piece(c, k, source(k)).wait_recv()
    total = send[me]
    for k in range(1, n_sim):
        total = total + recv[source(k)]
    acc[...] = total
    wide = lax.broadcasted_iota(jnp.int32, (half, 2 * width), 1) < width
    first, second = [], []
    for v in range(0, vb, 2):
        even, odd = acc[:, v, :], acc[:, v + 1, :]
        first.append(jnp.where(wide, even, pltpu.roll(odd, width, 1)))
        second.append(jnp.where(wide, pltpu.roll(even, width, 1), odd))
    comoment = extra + jnp.concatenate(
        [jnp.concatenate(first, axis=1), jnp.concatenate(second, axis=1)], axis=0
    )
    group_co = dot(member, comoment + spread)
    for j in range(n_sim):
        psend[j] = group_co[j:j + 1]
    sec_co = jnp.sum(group_co + sec_extra, axis=0, keepdims=True)
    gbuf[sec * n_sim + me] = jnp.concatenate(
        [sec_co, sec_mean, jnp.broadcast_to(sec_count, (1, width))], axis=1
    )
    for a, k in others:
        global_piece(a, k, sec * n_sim + me).start()
    for k in range(1, n_sim):
        group_piece(k, me).start()
    cov_out[...] = comoment / (number - 1.0)
    prec[me] = psend[me]

    mine = lax.broadcasted_iota(jnp.int32, (n_sim, 1), 0) == me
    my_count = jnp.sum(jnp.where(mine, group_count, 0.0), axis=0, keepdims=True)
    for a, k in others:
        global_piece(a, k, back(a) * n_sim + source(k)).wait_recv()
    for k in range(1, n_sim):
        group_piece(k, source(k)).wait_recv()
    divisor = jnp.maximum(my_count - 1.0, 1.0)
    for j in range(n_sim):
        gcov_out[:, j * flat:(j + 1) * flat] = prec[j] / divisor

    heads = [gbuf[a * n_sim][:, flat:] for a in range(n_sec)]
    sec_means = jnp.concatenate([h[:, :width] for h in heads], axis=0)
    sec_counts = jnp.concatenate([h[:, width:] for h in heads], axis=0)
    all_count = jnp.sum(sec_counts, axis=0, keepdims=True)
    global_mean = jnp.sum(sec_counts * sec_means, axis=0, keepdims=True) / all_count
    gmean_out[...] = global_mean
    gap = sec_means - global_mean
    between = lax.dot_general(
        sec_counts * gap, gap, (((0,), (0,)), ((), ())), precision=HIGH,
        preferred_element_type=jnp.float32,
    )
    parts = []
    for j in range(n_sim):
        parts.append(sum(gbuf[a * n_sim + j][:, :flat] for a in range(n_sec)))
    stack = jnp.concatenate(parts, axis=0)
    for v in range(0, vb, 2):
        both = stack[:, v * width:(v + 2) * width]
        g64[pl.ds(v, n_sim, stride=vb), :] = both
        g64[pl.ds(v + 1, n_sim, stride=vb), :] = pltpu.roll(both, width, 1)
    glob_out[...] = (g64[:, :width] + between) / (all_count - 1.0)

    for k in range(1, n_sim):
        means(k, me).wait_send()
        group_piece(k, me).wait_send()
        for c in range(chunks):
            piece(c, k, me).wait_send()
    for a, k in others:
        global_piece(a, k, sec * n_sim + me).wait_send()


def local(state, owner, counts):
    slabs, width, cells = state.shape
    n_sim = lax.axis_size("sim")
    n_sec = lax.axis_size("section")
    n_dev = n_sec * n_sim
    vb = width // n_sim
    flat = vb * width
    half = slabs // 2
    chunks = 4
    f32 = jnp.float32
    vmem = pl.BlockSpec(memory_space=pltpu.VMEM)
    dma = pltpu.SemaphoreType.DMA
    slab_mean, slab_cov, group_cov, global_mean, global_cov = pl.pallas_call(
        functools.partial(kernel, n_sec, n_sim, chunks),
        out_shape=(
            jax.ShapeDtypeStruct((slabs, width), f32),
            jax.ShapeDtypeStruct((slabs, flat), f32),
            jax.ShapeDtypeStruct((1, width * width), f32),
            jax.ShapeDtypeStruct((1, width), f32),
            jax.ShapeDtypeStruct((width, width), f32),
        ),
        in_specs=[
            pl.BlockSpec(memory_space=pl.ANY),
            pl.BlockSpec(memory_space=pltpu.SMEM),
            vmem,
            vmem,
        ],
        out_specs=(vmem,) * 5,
        scratch_shapes=[
            pltpu.VMEM((slabs, width, cells), f32),
            pltpu.VMEM((n_sim, half, vb, 2 * width), f32),
            pltpu.VMEM((n_sim, half, vb, 2 * width), f32),
            pltpu.VMEM((half, vb, 2 * width), f32),
            pltpu.VMEM((width, 2 * width), f32),
            pltpu.VMEM((n_sim, half, 2 * width), f32),
            pltpu.VMEM((n_sim, 1, flat), f32),
            pltpu.VMEM((n_sim, 1, flat), f32),
            pltpu.VMEM((n_dev, 1, flat + 2 * width), f32),
            pltpu.VMEM((width, 2 * width), f32),
            dma((chunks, 2)),
            dma((chunks, n_sim)),
            dma((chunks, n_sim)),
            dma((n_sim,)),
            dma((n_sim,)),
            dma((n_sim,)),
            dma((n_sim,)),
            dma((n_dev,)),
            dma((n_dev,)),
        ],
        compiler_params=pltpu.CompilerParams(collective_id=0, has_side_effects=True),
    )(state, counts, counts[:, None], owner)
    return (slab_mean, slab_cov, group_cov, global_mean.reshape(width), global_cov)


def solution(mesh):
    return jax.shard_map(
        local,
        mesh=mesh,
        in_specs=(P("section", None, "sim"), P("section", None), P("section")),
        out_specs=(P("section", None), P("section", "sim"), P(("section", "sim"), None), P(), P()),
        check_vma=False,
    )
```

time: 162 us -> 41.2 us (0.25)
  blocking collectives: 81.6 us -> 0 us
  Pallas kernels: 0 us -> 30.7 us
  starting transfers between devices: 25.5 us -> 0 us
  matrix products: 16.5 us -> 0 us
  other arithmetic: 13.4 us -> 0 us
  waiting for transfers between devices: 11.3 us -> 0 us
  between operations: 2.71 us -> 0.64 us
    psum x2 -> x0, blocking collectives: 81.6 us -> none  [the longest x1 41.6 us: local(): lax.psum((group_count, group_count * group_mean), ('section', 'sim'))]
    pallas_call x0 -> x1, Pallas kernels: none -> 30.7 us  [local(): pl.pallas_call(functools.partial(kernel, n_sec, n_sim, chunks), out_shape...]
    all_to_all x5 -> x0, starting transfers between devices: 25.5 us -> none  [the longest x1 7.28 us: local(): lax.all_to_all(send_count, 'sim', split_axis=0, concat_axis=0, tiled=True)]
    dot_general x3 -> x0, matrix products: 16.5 us -> none  [the longest x1 14.9 us: local(): jnp.einsum('svc,swc->svw', centered, centered, precision=high)]
    all_to_all x5 -> x0, waiting for transfers between devices: 11.3 us -> none  [the longest x1 5.96 us: local(): lax.all_to_all(send_mean, 'sim', split_axis=0, concat_axis=0, tiled=True)]
    unnamed x5 -> x6, local copies, waits for them, and re-layouts: 1.55 us -> 8.01 us
    reduce_sum x7 -> x0, other arithmetic: 5.94 us -> none  [the longest x1 4.11 us: local(): jnp.sum(jnp.where(live[:, None, :], state, 0.0), axis=2)]
    gather x5 -> x0, local copies, waits for them, and re-layouts: 4.72 us -> none  [the longest x1 1.24 us: local(): slab_cov = back_cov[slot_of, 0]]
  transfers between devices with their start and end apart: 5 -> 0, of which waited for: 2 -> 0; matrix products, arithmetic and copies ran while one was open for 19% -> 0% of each run, Pallas kernels for 0% -> 0%
where the time goes in v1:
time: 41.2 us; the launch traced here: 40.7 us
  Pallas kernels  30.7 us (75%)
  local copies, waits for them, and re-layouts  9.35 us (23%)
  between operations  0.64 us (2%)
    pallas_call x1, Pallas kernels, local(): pl.pallas_call(functools.partial(kernel, n_sec, n_sim, chunks), out_shape...  30.7 us
    unnamed x6, local copies, waits for them, and re-layouts  8.01 us
    broadcast_in_dim x1, local copies, waits for them, and re-layouts, local(): counts[:, None]  1.34 us

profile of v1, /device:TPU:0, one launch (start us, length us, event | category | flops | bytes accessed | tf_op | source)
XLA Modules:
  0.0 40.7 jit_solution(6078046220661577227)
XLA Ops:
  0.6 1.3 %copy.9.owner_v = s32[32,1]{1,0:T(8,128)} copy(s32[32,1]{0,1:T(1,128)} %param.4) | data formatting | bytes 256 | tf_op args[1]
  2.0 1.3 %copy.8.counts_v = s32[32,1]{1,0:T(8,128)} copy(s32[32,1]{0,1:T(1,128)} %bitcast.2) | data formatting | bytes 256 | tf_op jit(solution)/shard_map/broadcast_in_dim | solution.py:296
  3.3 30.7 %shard_map.74 = (f32[32,64]{1,0:T(8,128)}, f32[32,512]{1,0:T(8,128)}, f32[1,4096]{1,0:T(1,128)}, f32[1,64]{1,0:T(1,128)}, f32[64,64]{1,0:T(8,128)}) custom-call(f32[32,64,1024]{2,1,0:T(8,128)} %state.1, s32[32]{0:T(128)} %counts_s.1, s32[32,1]{1,0:T(8,128)} %copy.8.counts_v, s32[32,1]{1,0:T(8,128)} %copy.9.owner_v), custom_call_target="tpu_custom_call" | custom-call | tf_op jit(solution)/shard_map/pallas_call | solution.py:258
  34.1 1.3 %copy.15 = f32[32,64]{1,0:T(8,128)} copy(f32[32,64]{1,0:T(8,128)} %get-tuple-element.20) | data formatting | bytes 16384
  35.4 1.5 %copy.16 = f32[32,512]{1,0:T(8,128)} copy(f32[32,512]{1,0:T(8,128)} %get-tuple-element.21) | data formatting | bytes 131072
  36.9 1.3 %copy.17 = f32[1,4096]{1,0:T(1,128)} copy(f32[1,4096]{1,0:T(1,128)} %get-tuple-element.22) | data formatting | bytes 32768
  38.2 1.2 %copy.18 = f32[64]{0:T(128)} copy(f32[64]{0:T(128)} %bitcast.3) | data formatting | bytes 512
  39.4 1.4 %copy.19 = f32[64,64]{1,0:T(8,128)} copy(f32[64,64]{1,0:T(8,128)} %get-tuple-element.24) | data formatting | bytes 32768

commit v2 on v1

--- a/solution.py
+++ b/solution.py
@@ -21,7 +21,7 @@
 
 def kernel(
     n_sec, n_sim, chunks,
-    state, counts_s, counts_v, owner_v,
+    state, counts_s, counts_r, owner_r,
     mean_out, cov_out, gcov_out, gmean_out, glob_out,
     x, send, recv, acc, mt, mrec, psend, prec, gbuf, g64,
     in_sem, s1, r1, sm, rm, sp, rp, sg, rg,
@@ -133,17 +133,22 @@
         for k in range(1, n_sim):
             piece(c, k, me).start()
 
-    counts = counts_v[...]
-    number = counts.astype(jnp.float32)
-    owner = owner_v[...]
+    across = lax.broadcasted_iota(jnp.int32, (slabs, slabs), 1)
+    down = lax.broadcasted_iota(jnp.int32, (slabs, slabs), 0)
+
+    def upright(row):
+        return jnp.sum(jnp.where(across == down, row, 0.0), axis=1, keepdims=True)
+
+    number = upright(counts_r[...].astype(jnp.float32))
+    owner_row = owner_r[...].astype(jnp.float32)
+    owner = upright(owner_row)
     spot = lax.broadcasted_iota(jnp.int32, (width, flat), 1)
     line = lax.broadcasted_iota(jnp.int32, (width, flat), 0)
     choose = (line == me * vb + spot // width).astype(jnp.float32)
-    owner_rows = jnp.transpose(jnp.broadcast_to(owner.astype(jnp.float32), (slabs, 128)))
     name = lax.broadcasted_iota(jnp.int32, (n_sim, slabs), 0)
-    member = (owner_rows[:n_sim] == name.astype(jnp.float32)).astype(jnp.float32)
+    member = (owner_row == name.astype(jnp.float32)).astype(jnp.float32)
     column = lax.broadcasted_iota(jnp.int32, (slabs, n_sim), 1)
-    member_t = (owner == column).astype(jnp.float32)
+    member_t = (owner == column.astype(jnp.float32)).astype(jnp.float32)
 
     for k in range(1, n_sim):
         means(k, source(k)).wait_recv()
@@ -151,7 +156,7 @@
     for j in range(n_sim):
         packed = mrec[j]
         tiles.append(jnp.concatenate([packed[:, :width], packed[:, width:]], axis=0))
-        amounts.append(jnp.clip(counts - j * cells, 0, cells).astype(jnp.float32))
+        amounts.append(jnp.clip(number - float(j * cells), 0.0, float(cells)))
     mean = sum(n * t for n, t in zip(amounts, tiles)) / number
     mean_out[...] = mean
     gaps = [t - mean for t in tiles]
@@ -241,6 +246,11 @@
             piece(c, k, me).wait_send()
     for a, k in others:
         global_piece(a, k, sec * n_sim + me).wait_send()
+
+
+def hand_over(*refs):
+    for src, dst in zip(refs[:len(refs) // 2], refs[len(refs) // 2:]):
+        dst[...] = src[...]
 
 
 def local(state, owner, counts):
@@ -255,15 +265,16 @@
     f32 = jnp.float32
     vmem = pl.BlockSpec(memory_space=pltpu.VMEM)
     dma = pltpu.SemaphoreType.DMA
-    slab_mean, slab_cov, group_cov, global_mean, global_cov = pl.pallas_call(
+    shapes = (
+        jax.ShapeDtypeStruct((slabs, width), f32),
+        jax.ShapeDtypeStruct((slabs, flat), f32),
+        jax.ShapeDtypeStruct((1, width * width), f32),
+        jax.ShapeDtypeStruct((1, width), f32),
+        jax.ShapeDtypeStruct((width, width), f32),
+    )
+    results = pl.pallas_call(
         functools.partial(kernel, n_sec, n_sim, chunks),
-        out_shape=(
-            jax.ShapeDtypeStruct((slabs, width), f32),
-            jax.ShapeDtypeStruct((slabs, flat), f32),
-            jax.ShapeDtypeStruct((1, width * width), f32),
-            jax.ShapeDtypeStruct((1, width), f32),
-            jax.ShapeDtypeStruct((width, width), f32),
-        ),
+        out_shape=shapes,
         in_specs=[
             pl.BlockSpec(memory_space=pl.ANY),
             pl.BlockSpec(memory_space=pltpu.SMEM),
@@ -293,7 +304,13 @@
             dma((n_dev,)),
         ],
         compiler_params=pltpu.CompilerParams(collective_id=0, has_side_effects=True),
-    )(state, counts, counts[:, None], owner)
+    )(state, counts, counts.reshape(1, slabs), owner.reshape(1, slabs))
+    slab_mean, slab_cov, group_cov, global_mean, global_cov = pl.pallas_call(
+        hand_over,
+        out_shape=shapes,
+        in_specs=[vmem] * 5,
+        out_specs=(vmem,) * 5,
+    )(*results)
     return (slab_mean, slab_cov, group_cov, global_mean.reshape(width), global_cov)
 
 

time: 41.2 us -> 33 us (0.80)
  local copies, waits for them, and re-layouts: 9.35 us -> 0 us
  Pallas kernels: 30.7 us -> 32.2 us
    unnamed x6 -> x0, local copies, waits for them, and re-layouts: 8.01 us -> none
    pallas_call x0 -> x1, Pallas kernels: none -> 1.5 us  [local(): pl.pallas_call(hand_over, out_shape=shapes, in_specs=[vmem] * 5, out_spec...]
    broadcast_in_dim x1 -> x0, local copies, waits for them, and re-layouts: 1.34 us -> none  [local(): counts[:, None]]
where the time goes in v2:
time: 33 us; the launch traced here: 32.8 us
  Pallas kernels  32.2 us (98%)
  between operations  0.64 us (2%)
    pallas_call x1, Pallas kernels, local(): pl.pallas_call(functools.partial(kernel, n_sec, n_sim, chunks), out_shape...  30.7 us
    pallas_call x1, Pallas kernels, local(): pl.pallas_call(hand_over, out_shape=shapes, in_specs=[vmem] * 5, out_spec...  1.5 us

profile of v2, /device:TPU:0, one launch (start us, length us, event | category | flops | bytes accessed | tf_op | source)
XLA Modules:
  0.0 32.8 jit_solution(15617296220467785954)
XLA Ops:
  0.6 30.7 %shard_map.74 = (f32[32,64]{1,0:T(8,128)}, f32[32,512]{1,0:T(8,128)}, f32[1,4096]{1,0:T(1,128)}, f32[1,64]{1,0:T(1,128)}, f32[64,64]{1,0:T(8,128)}) custom-call(f32[32,64,1024]{2,1,0:T(8,128)} %state.1, s32[32]{0:T(128)} %counts_s.1, s32[1,32]{1,0:T(1,128)} %bitcast.3, s32[1,32]{1,0:T(1,128)} %bitcast.4), custom_call_target="tpu_custom_call" | custom-call | tf_op jit(solution)/shard_map/pallas_call | solution.py:275
  31.3 1.5 %shard_map.75 = (f32[32,64]{1,0:T(8,128)}, f32[32,512]{1,0:T(8,128)}, f32[1,4096]{1,0:T(1,128)}, f32[1,64]{1,0:T(1,128)}, f32[64,64]{1,0:T(8,128)}) custom-call(f32[32,64]{1,0:T(8,128)} %get-tuple-element.15.refs_0_, f32[32,512]{1,0:T(8,128)} %get-tuple-element.16.refs_1_, f32[1,4096]{1,0:T(1,128)} %get-tuple-element.17.refs_2_, ...), custom_call_target="tpu_custom_call" | custom-call | tf_op jit(solution)/shard_map/pallas_call | solution.py:308

commit v3 on v2

--- a/solution.py
+++ b/solution.py
@@ -130,7 +130,7 @@
             mrec[me] = jnp.concatenate([rows[:half], rows[half:slabs]], axis=1)
             for k in range(1, n_sim):
                 means(k, me).start()
-        for k in range(1, n_sim):
+        for k in sorted(range(1, n_sim), key=lambda k: -min(k, n_sim - k)):
             piece(c, k, me).start()
 
     across = lax.broadcasted_iota(jnp.int32, (slabs, slabs), 1)

time: 33 us -> 32.6 us (0.988)
  Pallas kernels: 32.2 us -> 31.8 us
    pallas_call x1, Pallas kernels: 30.7 us -> 30.3 us  [local(): pl.pallas_call(functools.partial(kernel, n_sec, n_sim, chunks), out_shape...]
where the time goes in v3:
time: 32.6 us; the launch traced here: 32.5 us
  Pallas kernels  31.8 us (98%)
  between operations  0.64 us (2%)
    pallas_call x1, Pallas kernels, local(): pl.pallas_call(functools.partial(kernel, n_sec, n_sim, chunks), out_shape...  30.3 us
    pallas_call x1, Pallas kernels, local(): pl.pallas_call(hand_over, out_shape=shapes, in_specs=[vmem] * 5, out_spec...  1.5 us

profile of v3, /device:TPU:0, one launch (start us, length us, event | category | flops | bytes accessed | tf_op | source)
XLA Modules:
  0.0 32.5 jit_solution(9629938978194830471)
XLA Ops:
  0.6 30.3 %shard_map.74 = (f32[32,64]{1,0:T(8,128)}, f32[32,512]{1,0:T(8,128)}, f32[1,4096]{1,0:T(1,128)}, f32[1,64]{1,0:T(1,128)}, f32[64,64]{1,0:T(8,128)}) custom-call(f32[32,64,1024]{2,1,0:T(8,128)} %state.1, s32[32]{0:T(128)} %counts_s.1, s32[1,32]{1,0:T(1,128)} %bitcast.3, s32[1,32]{1,0:T(1,128)} %bitcast.4), custom_call_target="tpu_custom_call" | custom-call | tf_op jit(solution)/shard_map/pallas_call | solution.py:275
  31.0 1.5 %shard_map.75 = (f32[32,64]{1,0:T(8,128)}, f32[32,512]{1,0:T(8,128)}, f32[1,4096]{1,0:T(1,128)}, f32[1,64]{1,0:T(1,128)}, f32[64,64]{1,0:T(8,128)}) custom-call(f32[32,64]{1,0:T(8,128)} %get-tuple-element.15.refs_0_, f32[32,512]{1,0:T(8,128)} %get-tuple-element.16.refs_1_, f32[1,4096]{1,0:T(1,128)} %get-tuple-element.17.refs_2_, ...), custom_call_target="tpu_custom_call" | custom-call | tf_op jit(solution)/shard_map/pallas_call | solution.py:308
